TPU v7x, 256 devices: a 4x2x16 block of a 4x16x16 slice. The times are simulated.
256 devices in a mesh: tracts: 2 (over y), sky: 32 (over z, core), depth: 4 (over x).
Axes of the slice: x: 4, y: 2, z: 16, core: 2. Of those that a mesh axis runs over, the one named last changes fastest.
The devices are a block of a 4x16x16 slice.
Arguments:
- visit_tiles: bfloat16 [1024, 32, 64, 512], P(('tracts', 'sky', 'depth')), parts along dimension 0, may hold values from -6 to 6
- warp_matrix: bfloat16 [1024, 512, 512], P(('tracts', 'sky', 'depth')), parts along dimension 0, may hold values from -0.25 to 0.25
- flux_scale: float32 [1024], P(('tracts', 'sky', 'depth')), parts along dimension 0, may hold values from 0.3 to 3
- patch_lists: int32 [1024, 32], P(('tracts', 'sky', 'depth')), parts along dimension 0, may hold values from 0 to 127, all different within a row; in each aligned block of 4 rows (0 to 3, 4 to 7, ...) at most 2 rows name the same one
- clip_bits: int32 [1024, 32, 4, 512], P(('tracts', 'sky', 'depth')), parts along dimension 0, may hold values from -2147483648 to 2147483647, as said below
Outputs:
- coadd_mean: float32 [2, 256, 64, 512], P(None, ('tracts', 'sky'), 'depth'), parts along dimension 1
- coadd_var: float32 [2, 256, 64, 512], P(None, ('tracts', 'sky'), 'depth'), parts along dimension 1
There are 2 independent parts, one for each index of `tracts`. A program takes and returns all parts, laid end to end along the dimension named above; each array names one. Nothing has to cross between parts.
Inputs may be any that keep to these rules, and one draw needn't show every extreme that they name: `patch_lists`: row v names the 32 different patches of visit v's blocks. In the rows of one device no patch is named more than 2 times, a bound that some block reaches there; every patch is named by some row. Bit 16 t + j of clip_bits[v, k, g, c] is 1 when clip pass t (t = 0 or 1) keeps the sample of visit v's block k at row 16 g + j, column c.
All inputs are finite; a program needn't handle non-finite values.
Results may differ from a plain program's by a relative error of at most 0.0029.
Values may be sent and summed in bfloat16 or wider, within the bound.
A program may use at most 128 MiB of HBM per device.

v0:
```python
import jax
import jax.numpy as jnp
from jax import lax
from jax.sharding import PartitionSpec as P

PATCH_DEV = 4
CAPACITY = 2


def unpack_keep(packed, offset):
    positions = jnp.arange(16, dtype=jnp.int32) + offset
    bit_flags = jnp.bitwise_and(jnp.right_shift(packed[..., None, :], positions[:, None]), 1)
    target_shape = packed.shape[:-2] + (packed.shape[-2] * 16, packed.shape[-1])
    return bit_flags.reshape(target_shape).astype(jnp.float32)


def finish(count_first, sum_first, square_first, count_both, shift_sum, shift_square):
    first_mean = sum_first / jnp.maximum(count_first, 1.0)
    first_var = (square_first - sum_first * first_mean) / jnp.maximum(count_first - 1.0, 1.0)
    final_mean = first_mean + shift_sum / jnp.maximum(count_both, 1.0)
    final_var = (shift_square - shift_sum * shift_sum / jnp.maximum(count_both, 1.0)) / jnp.maximum(
        count_both - 1.0, 1.0
    )
    return (jnp.stack([first_mean, final_mean]), jnp.stack([first_var, final_var]))


def first_sums(samples, keep_first):
    count_first = jnp.sum(keep_first, axis=(0, 2))
    sum_first = jnp.sum(keep_first * samples, axis=(0, 2))
    square_first = jnp.sum(keep_first * samples * samples, axis=(0, 2))
    return (count_first, sum_first, square_first)


def stack_rows(pieces):
    received, packed = pieces
    samples = received.astype(jnp.float32)
    keep_first = unpack_keep(packed, 0)
    keep_both = keep_first * unpack_keep(packed, 16)
    count_first, sum_first, square_first = first_sums(samples, keep_first)
    first_mean = sum_first / jnp.maximum(count_first, 1.0)
    centred = samples - first_mean[None, :, None]
    count_both = jnp.sum(keep_both, axis=(0, 2))
    shift_sum = jnp.sum(keep_both * centred, axis=(0, 2))
    shift_square = jnp.sum(keep_both * centred * centred, axis=(0, 2))
    return finish(count_first, sum_first, square_first, count_both, shift_sum, shift_square)


def per_device(visit_tiles, warp_matrix, flux_scale, patch_lists, clip_bits):
    visits_here, intersections_here, block_rows, columns = visit_tiles.shape
    entries = visits_here * intersections_here
    sky_size = lax.axis_size("sky")
    depth_size = lax.axis_size("depth")
    patches = PATCH_DEV * sky_size
    warped = jnp.einsum(
        "vkrc,vcf->vkrf", visit_tiles, warp_matrix, preferred_element_type=jnp.float32
    )
    warped = (warped * flux_scale[:, None, None, None]).astype(jnp.bfloat16)
    targets = patch_lists.reshape(entries)
    onehot = (targets[:, None] == jnp.arange(patches, dtype=jnp.int32)[None, :]).astype(jnp.int32)
    earlier = jnp.cumsum(onehot, axis=0) - onehot
    slot_rank = jnp.sum(earlier * onehot, axis=1)
    source = jnp.full((patches * CAPACITY,), entries, jnp.int32)
    source = source.at[targets * CAPACITY + slot_rank].set(jnp.arange(entries, dtype=jnp.int32))
    rows_share = block_rows // depth_size
    depth_ids = jnp.arange(depth_size, dtype=jnp.int32)
    gather_index = (
        source.reshape(sky_size, 1, PATCH_DEV * CAPACITY) * depth_size + depth_ids[None, :, None]
    )
    send_tiles = jnp.take(
        warped.reshape(entries * depth_size, rows_share, columns),
        gather_index,
        axis=0,
        mode="fill",
        fill_value=0,
    )
    send_bits = jnp.take(
        clip_bits.reshape(entries * depth_size, rows_share // 16, columns),
        gather_index,
        axis=0,
        mode="fill",
        fill_value=0,
    )
    send_tiles = send_tiles.reshape(sky_size * depth_size, PATCH_DEV, CAPACITY, rows_share, columns)
    send_bits = send_bits.reshape(
        sky_size * depth_size, PATCH_DEV, CAPACITY, rows_share // 16, columns
    )
    mean_out, var_out = stack_rows(
        (
            lax.all_to_all(send_tiles, ("sky", "depth"), split_axis=0, concat_axis=0, tiled=True),
            lax.all_to_all(send_bits, ("sky", "depth"), split_axis=0, concat_axis=0, tiled=True),
        )
    )
    return (mean_out, var_out)


def solution(mesh):
    placed = (
        P(("tracts", "sky", "depth"), None, None, None),
        P(("tracts", "sky", "depth"), None, None),
        P(("tracts", "sky", "depth")),
        P(("tracts", "sky", "depth"), None),
        P(("tracts", "sky", "depth"), None, None, None),
    )
    return jax.shard_map(
        per_device,
        mesh=mesh,
        in_specs=placed,
        out_specs=(
            P(None, ("tracts", "sky"), "depth", None),
            P(None, ("tracts", "sky"), "depth", None),
        ),
        check_vma=False,
    )
```

profile of v0, /device:TPU:33, one launch (start us, length us, event | category | flops | bytes accessed | tf_op | source)
XLA Modules:
  0.0 913.9 jit_solution(7155397547654130632)
XLA Ops:
  0.6 0.9 eq.15
  1.6 0.7 broadcast_multiply_fusion
  2.3 0.2 reduce_window_sum.11
  2.5 0.2 select_reduce_fusion
  2.8 1.0 scatter_custom_fusion
  4.0 0.1 reshape.225
  4.2 0.1 add.123
  4.3 0.1 add.125
  4.4 0.2 copy.11
  4.6 1.6 reshape.221
  6.2 4.9 gather_fusion
  11.1 3.5 gather.13
  14.6 3.5 bitcast_select_fusion
  18.1 31.1 %all-to-all-start = ((s32[128,4,2,1,512]{4,2,1,3,0:T(2,128)}), s32[128,4,2,1,512]{4,2,1,3,0:T(2,128)}, u32[]{:S(2)}, u32[]{:S(2)}) async-start(s32[128,4,2,1,512]{4,2,1,3,0:T(2,128)} %bitcast_select_fusion), calls=%async_computation | async-start | bytes 4194304 | tf_op jit(solution)/shard_map/all_to_all | solution.py:90
  49.2 10.1 %multiply_convert_fusion = bf16[4,32,64,512]{3,2,1,0:T(8,128)(2,1)} fusion(bf16[4,32,64,512]{3,2,1,0:T(8,128)(2,1)} %param.5, f32[4]{0:T(128)S(1)} %copy-done.2, bf16[4,512,512]{2,1,0:T(8,128)(2,1)S(1)} %copy-done), kind=kOutput, calls=%fused_computation.16 | convolution fusion | flops 4303355904 | bytes 18874384 | tf_op jit(solution)/shard_map/vkrc,vcf->vkrf/dot_general | solution.py:54
  59.3 15.8 %gather_fusion.1 = bf16[1024,16,512]{2,1,0:T(8,128)(2,1)} fusion(bf16[512,16,512]{2,1,0:T(8,128)(2,1)} %bitcast.61, s32[1024]{0:T(1024)S(1)} %broadcast_clamp_fusion), kind=kCustom, calls=%fused_computation.1 | custom fusion | bytes 33558528 | tf_op jit(solution)/shard_map/jit(_take)/gather | solution.py:69
  75.1 14.0 %broadcast_select_fusion = bf16[128,4,2,16,512]{4,3,2,1,0:T(8,128)(2,1)} fusion(bf16[128,4,2,16,512]{4,3,2,1,0:T(8,128)(2,1)} %bitcast.60, pred[128,4,2]{2,1,0:T(4,128)(4,1)S(1)} %copy.11), kind=kLoop, calls=%fused_computation.17 | loop fusion | flops 8388608 | bytes 33555456 | tf_op jit(solution)/shard_map/jit(_take)/select_n | solution.py:69
  89.1 58.0 %all-to-all-done = s32[128,4,2,1,512]{4,2,1,3,0:T(2,128)} async-done(((s32[128,4,2,1,512]{4,2,1,3,0:T(2,128)}), s32[128,4,2,1,512]{4,2,1,3,0:T(2,128)}, u32[]{:S(2)}, u32[]{:S(2)}) %all-to-all-start) | async-done | bytes 2097184 | tf_op jit(solution)/shard_map/all_to_all | solution.py:90
  147.1 9.9 %all-to-all-start.1 = ((bf16[128,4,2,16,512]{4,3,2,1,0:T(8,128)(2,1)}), bf16[128,4,2,16,512]{4,3,2,1,0:T(8,128)(2,1)}, u32[]{:S(2)}, u32[]{:S(2)}) async-start(bf16[128,4,2,16,512]{4,3,2,1,0:T(8,128)(2,1)} %broadcast_select_fusion), calls=%async_computation.1 | async-start | bytes 33554432 | tf_op jit(solution)/shard_map/all_to_all | solution.py:89
  157.0 724.7 %all-to-all-done.1 = bf16[128,4,2,16,512]{4,3,2,1,0:T(8,128)(2,1)} async-done(((bf16[128,4,2,16,512]{4,3,2,1,0:T(8,128)(2,1)}), bf16[128,4,2,16,512]{4,3,2,1,0:T(8,128)(2,1)}, u32[]{:S(2)}, u32[]{:S(2)}) %all-to-all-start.1) | async-done | bytes 16777248 | tf_op jit(solution)/shard_map/all_to_all | solution.py:89
  881.7 10.6 %convert_reduce_fusion = (f32[4,16,512]{2,1,0:T(8,128)S(1)}, f32[4,16,512]{2,1,0:T(8,128)S(1)}) fusion(s32[128,4,2,512]{3,2,1,0:T(2,128)} %bitcast.3, bf16[128,4,2,16,512]{4,3,2,1,0:T(8,128)(2,1)} %all-to-all-done.1), kind=kLoop, calls=%fused_computation.11 | loop fusion | flops 58654720 | bytes 19136512 | tf_op jit(solution)/shard_map/reduce_sum | solution.py:28
  892.4 20.6 %fusion.2 = (f32[4,16,512]{2,1,0:T(8,128)S(1)}, f32[4,16,512]{2,1,0:T(8,128)S(1)}, f32[4,16,512]{2,1,0:T(8,128)S(1)}, f32[4,16,512]{2,1,0:T(8,128)S(1)}) fusion(bf16[128,4,2,16,512]{4,3,2,1,0:T(8,128)(2,1)} %all-to-all-done.1, f32[4,16,512]{2,1,0:T(8,128)S(1)} %maximum_divide_fusion, s32[16]{0:T(128)S(1)} %iota_add_fusion, s32[128,4,2,512]{3,2,1,0:T(2,128)} %bitcast.3), kind=kLoop, calls=%fused_computation.8 | loop fusion | flops 142475264 | bytes 19529792 | tf_op jit(solution)/shard_map/reduce_sum | solution.py:44
  913.0 0.1 bitcast_divide_fusion.1
  913.1 0.8 pad_maximum_fusion
  (20 shorter events, 0.5 us)
Async XLA Ops:
  0.6 48.6 %copy-start = (bf16[4,512,512]{2,1,0:T(8,128)(2,1)S(1)}, bf16[4,512,512]{2,1,0:T(8,128)(2,1)}, u32[]{:S(2)}) copy-start(bf16[4,512,512]{2,1,0:T(8,128)(2,1)} %param.6) | copy-start | bytes 6291460
  4.6 44.6 %copy-start.2 = (f32[4]{0:T(128)S(1)}, f32[4]{0:T(128)}, u32[]{:S(2)}) copy-start(f32[4]{0:T(128)} %param.7) | copy-start | bytes 52
  18.1 129.0 %all-to-all-start = ((s32[128,4,2,1,512]{4,2,1,3,0:T(2,128)}), s32[128,4,2,1,512]{4,2,1,3,0:T(2,128)}, u32[]{:S(2)}, u32[]{:S(2)}) async-start(s32[128,4,2,1,512]{4,2,1,3,0:T(2,128)} %bitcast_select_fusion), calls=%async_computation | async-start | bytes 4194304 | tf_op jit(solution)/shard_map/all_to_all | solution.py:90
  147.1 734.6 %all-to-all-start.1 = ((bf16[128,4,2,16,512]{4,3,2,1,0:T(8,128)(2,1)}), bf16[128,4,2,16,512]{4,3,2,1,0:T(8,128)(2,1)}, u32[]{:S(2)}, u32[]{:S(2)}) async-start(bf16[128,4,2,16,512]{4,3,2,1,0:T(8,128)(2,1)} %broadcast_select_fusion), calls=%async_computation.1 | async-start | bytes 33554432 | tf_op jit(solution)/shard_map/all_to_all | solution.py:89
  881.7 32.2 %copy-start.1 = (bf16[4,512,512]{2,1,0:T(8,128)(2,1)S(1)}, bf16[4,512,512]{2,1,0:T(8,128)(2,1)}, u32[]{:S(2)}) copy-start(bf16[4,512,512]{2,1,0:T(8,128)(2,1)} %param.6) | copy-start | bytes 6291460
where the time goes:
time: 914 us
  waiting for transfers between devices  783 us (86%)
  other arithmetic  50.9 us (6%)
  starting transfers between devices  40.9 us (4%)
  local copies, waits for them, and re-layouts  28.5 us (3%)
  matrix products  10.1 us (1%)
    all_to_all x1, waiting for transfers between devices, per_device(): lax.all_to_all(send_tiles, ('sky', 'depth'), split_axis=0, concat_axis=0,...  725 us
    all_to_all x1, waiting for transfers between devices, per_device(): lax.all_to_all(send_bits, ('sky', 'depth'), split_axis=0, concat_axis=0,...  58 us
    all_to_all x1, starting transfers between devices, per_device(): lax.all_to_all(send_bits, ('sky', 'depth'), split_axis=0, concat_axis=0,...  31.1 us
    reduce_sum x1, other arithmetic, stack_rows(): shift_square = jnp.sum(keep_both * centred * centred, axis=(0, 2))  20.6 us
  transfers between devices with their start and end apart: 2, of which 2 were waited for; matrix products, arithmetic and copies ran while one was open for 4% of the time, Pallas kernels for 0%

commit v1 on v0

v1 whole, which is shorter than its diff:
```python
import functools

import jax
import jax.numpy as jnp
from jax import lax
from jax.experimental import pallas as pl
from jax.experimental.pallas import tpu as pltpu
from jax.sharding import PartitionSpec as P

PATCH_DEV = 4
CAPACITY = 2
CORES = 2
LANES = 128
FIELDS = 5
COUNT_UNIT = 4096.0
MESH = pl.DeviceIdType.MESH


def kernel_body(
    dims,
    tiles_hbm,
    warp_hbm,
    flux,
    bits_hbm,
    table_hbm,
    mean_out,
    var_out,
    tiles,
    warp,
    table_v,
    table,
    *refs,
):
    visits, blocks, rows, columns, xs, zs = dims
    entries = visits * blocks
    share = rows // xs
    chunks = columns // LANES
    half = zs // 2
    x_send, x_recv, bits = refs[:chunks], refs[chunks : 2 * chunks], refs[2 * chunks : 3 * chunks]
    (
        parts,
        parts_last,
        pair_recv,
        pair_recv_last,
        ring_send,
        ring_recv,
        load_sem,
        table_sem,
        own_sem,
        x_ssem,
        x_rsem,
        bits_ssem,
        bits_rsem,
        pair_ssem,
        pair_rsem,
        ring_ssem,
        ring_rsem,
    ) = refs[3 * chunks :]
    tract = lax.axis_index("tracts")
    sky = lax.axis_index("sky")
    x = lax.axis_index("depth")
    z, core = sky // CORES, lax.rem(sky, CORES)

    def x_peer(dx):
        return lax.rem(x + dx, xs)

    def z_peer(direction):
        step = 1 if direction == 0 else zs - 1
        return (tract, lax.rem(z + step, zs) * CORES + core, x)

    partner = (tract, z * CORES + (1 - core), x)

    barrier = pltpu.get_barrier_semaphore()
    greeted = [(tract, sky, x_peer(dx)) for dx in range(1, xs)]
    greeted += [z_peer(0), z_peer(1), partner]
    for device in greeted:
        pl.semaphore_signal(barrier, inc=1, device_id=device, device_id_type=MESH)

    def load_visit(v):
        return (
            pltpu.make_async_copy(tiles_hbm.at[v], tiles.at[v], load_sem.at[v, 0]),
            pltpu.make_async_copy(warp_hbm.at[v], warp.at[v], load_sem.at[v, 1]),
        )

    for v in range(visits):
        for copy in load_visit(v):
            copy.start()
    for j in range(chunks):
        for s in range(xs):
            x_recv[j][s, entries] = jnp.zeros((share, LANES), jnp.bfloat16)
            bits[j][s, pl.ds(entries, 8), :] = jnp.zeros((8, LANES), jnp.int32)
    pl.semaphore_wait(barrier, len(greeted))

    def table_copy(dx):
        return pltpu.make_async_remote_copy(
            src_ref=table_hbm,
            dst_ref=table_v.at[x],
            send_sem=table_sem.at[0, dx],
            recv_sem=table_sem.at[1, dx],
            device_id=(tract, sky, x_peer(dx)),
            device_id_type=MESH,
        )

    def bits_copy(j, dx):
        return pltpu.make_async_remote_copy(
            src_ref=bits_hbm.at[x_peer(dx), j],
            dst_ref=bits[j].at[x, pl.ds(0, entries)],
            send_sem=bits_ssem.at[j, dx],
            recv_sem=bits_rsem.at[j, dx],
            device_id=(tract, sky, x_peer(dx)),
            device_id_type=MESH,
        )

    def x_copy(j, v, dx):
        part = pl.ds(v * blocks, blocks)
        return pltpu.make_async_remote_copy(
            src_ref=x_send[j].at[x_peer(dx), part],
            dst_ref=x_recv[j].at[x, part],
            send_sem=x_ssem.at[j, v, dx],
            recv_sem=x_rsem.at[j, v, dx],
            device_id=(tract, sky, x_peer(dx)),
            device_id_type=MESH,
        )

    def own_bits(j):
        return pltpu.make_async_copy(
            bits_hbm.at[x, j], bits[j].at[x, pl.ds(0, entries)], own_sem.at[j, 0]
        )

    def own_rows(j):
        return pltpu.make_async_copy(
            x_send[j].at[x], x_recv[j].at[x, pl.ds(0, entries)], own_sem.at[j, 1]
        )

    own_table = pltpu.make_async_copy(table_hbm, table_v.at[x], table_sem.at[0, 0])
    own_table.start()
    for dx in range(1, xs):
        table_copy(dx).start()

    group = 8
    for j in range(chunks):
        own_bits(j).start()
        for dx in range(1, xs):
            bits_copy(j, dx).start()
        for v in range(visits):
            if j == 0:
                for copy in load_visit(v):
                    copy.wait()
            weights = warp[v, :, pl.ds(j * LANES, LANES)]
            scale = flux[v]

            def multiply(n, carry):
                first = pl.multiple_of(n * (group * rows), group * rows)
                product = jnp.dot(
                    tiles[v, pl.ds(first, group * rows), :],
                    weights,
                    preferred_element_type=jnp.float32,
                )
                scaled = (product * scale).astype(jnp.bfloat16)
                scaled = scaled.reshape(group, xs, share, LANES)
                at = pl.ds(v * blocks + n * group, group)
                for d in range(xs):
                    x_send[j][d, at] = scaled[:, d]
                return carry

            lax.fori_loop(0, blocks // group, multiply, 0)
            for dx in range(1, xs):
                x_copy(j, v, dx).start()
        own_rows(j).start()

    own_table.wait()
    for dx in range(1, xs):
        table_copy(dx).wait()
    to_scalar = pltpu.make_async_copy(table_v, table, table_sem.at[1, 0])
    to_scalar.start()
    to_scalar.wait()

    def wait_chunk(j):
        own_bits(j).wait()
        own_rows(j).wait()
        for dx in range(1, xs):
            bits_copy(j, dx).wait()
            for v in range(visits):
                x_copy(j, v, dx).wait()

    row = lax.broadcasted_iota(jnp.int32, (share, LANES), 0)
    mask_first = jnp.left_shift(jnp.int32(1), row)
    mask_both = jnp.bitwise_or(mask_first, jnp.left_shift(jnp.int32(1), row + 16))
    zero = jnp.zeros((share, LANES), jnp.float32)

    def patch_sums(j, patch):
        count, s1, q1, sb, qb = zero, zero, zero, zero, zero
        for s in range(xs):
            for r in range(CAPACITY):
                e = table[s, r, patch]
                sample = x_recv[j][s, e].astype(jnp.float32)
                word = bits[j][s, pl.ds(e, 1), :]
                first = jnp.bitwise_and(word, mask_first) != 0
                both = jnp.bitwise_and(word, mask_both) == mask_both
                kept = jnp.where(first, sample, 0.0)
                s1 = s1 + kept
                q1 = q1 + kept * kept
                kept = jnp.where(both, sample, 0.0)
                sb = sb + kept
                qb = qb + kept * kept
                count = count + jnp.where(
                    both, 1.0 + COUNT_UNIT, jnp.where(first, 1.0, 0.0)
                )
        return count, s1, q1, sb, qb

    def pair_copy(j, k):
        return pltpu.make_async_remote_copy(
            src_ref=parts.at[0],
            dst_ref=pair_recv.at[j, k],
            send_sem=pair_ssem.at[0],
            recv_sem=pair_rsem.at[j, k],
            device_id=partner,
            device_id_type=MESH,
        )

    def pair_copy_last(j):
        return pltpu.make_async_remote_copy(
            src_ref=parts_last.at[0],
            dst_ref=pair_recv_last.at[j],
            send_sem=pair_ssem.at[1],
            recv_sem=pair_rsem.at[j, half],
            device_id=partner,
            device_id_type=MESH,
        )

    def store_sums(dst, at, j, patch):
        for f, value in enumerate(patch_sums(j, patch)):
            dst[at[:-1] + (f, at[-1])] = value

    def partials(j, k):
        def side(w, outer):
            which = lax.rem(core + 1 + w, CORES)

            def one(n, inner):
                direction, i = n // PATCH_DEV, lax.rem(n, PATCH_DEV)
                moved = half + k * (2 * direction - 1)
                base = (lax.rem(z + moved, zs) * CORES + which) * PATCH_DEV
                store_sums(parts, (w, direction, i // 2, lax.rem(i, 2)), j, base + i)
                return inner

            lax.fori_loop(0, 2 * PATCH_DEV, one, 0)

            @pl.when(w == 0)
            def _():
                pair_copy(j, k).start()

            return outer

        lax.fori_loop(0, CORES, side, 0)

    def partials_last(j):
        def side(w, outer):
            base = (z * CORES + lax.rem(core + 1 + w, CORES)) * PATCH_DEV

            def one(i, inner):
                store_sums(parts_last, (w, i // 2, lax.rem(i, 2)), j, base + i)
                return inner

            lax.fori_loop(0, PATCH_DEV, one, 0)

            @pl.when(w == 0)
            def _():
                pair_copy_last(j).start()

            return outer

        lax.fori_loop(0, CORES, side, 0)

    def ring_copy(j, k, direction, h):
        return pltpu.make_async_remote_copy(
            src_ref=ring_send.at[lax.rem(k, 2), direction, h],
            dst_ref=ring_recv.at[j, k, direction, h],
            send_sem=ring_ssem.at[lax.rem(k, 2), direction, h],
            recv_sem=ring_rsem.at[j, k, direction, h],
            device_id=z_peer(direction),
            device_id_type=MESH,
        )

    def starts_at_zero(direction, h):
        return direction == h

    def tick(j, k, stage):
        pair_copy(j, k).wait()
        for h in range(2):
            for direction in range(2):
                if stage == 0 and not starts_at_zero(direction, h):
                    continue
                message = parts[1, direction, h] + pair_recv[j, k, direction, h]
                if stage == 2 or (stage == 1 and starts_at_zero(direction, h)):
                    ring_copy(j, k - 1, direction, h).wait()
                    message = message + ring_recv[j, k - 1, direction, h]
                ring_send[lax.rem(k, 2), direction, h] = message
                ring_copy(j, k, direction, h).start()

    def finish(j):
        pair_copy_last(j).wait()
        lanes = pl.ds(j * LANES, LANES)
        for h in range(2):
            total = parts_last[1, h] + pair_recv_last[j, h]
            for direction in range(2):
                if half > 1 or starts_at_zero(direction, h):
                    ring_copy(j, half - 1, direction, h).wait()
                    total = total + ring_recv[j, half - 1, direction, h]
            packed, s1, q1, sb, qb = (total[f] for f in range(FIELDS))
            count_both = jnp.floor(packed * (1.0 / COUNT_UNIT))
            count_first = packed - count_both * COUNT_UNIT
            first_mean = s1 / jnp.maximum(count_first, 1.0)
            first_var = (q1 - s1 * first_mean) / jnp.maximum(count_first - 1.0, 1.0)
            shift_sum = sb - first_mean * count_both
            shift_square = qb - first_mean * (sb + shift_sum)
            move = shift_sum / jnp.maximum(count_both, 1.0)
            final_var = (shift_square - shift_sum * move) / jnp.maximum(
                count_both - 1.0, 1.0
            )
            at = pl.ds(2 * h, 2)
            mean_out[0, at, :, lanes] = first_mean
            mean_out[1, at, :, lanes] = first_mean + move
            var_out[0, at, :, lanes] = first_var
            var_out[1, at, :, lanes] = final_var

    wait_chunk(0)
    partials(0, 0)

    for j in range(chunks):
        tick(j, 0, 0)
        if j > 0:
            finish(j - 1)
        if half > 1:
            partials(j, 1)
            tick(j, 1, 1)

            def later(k, carry):
                partials(j, k)
                tick(j, k, 2)
                return carry

            lax.fori_loop(2, half, later, 0)
        partials_last(j)
        if j < chunks - 1:
            wait_chunk(j + 1)
            partials(j + 1, 0)
    finish(chunks - 1)


def per_device(visit_tiles, warp_matrix, flux_scale, patch_lists, clip_bits):
    visits, blocks, rows, columns = visit_tiles.shape
    entries = visits * blocks
    xs = lax.axis_size("depth")
    skies = lax.axis_size("sky")
    zs = skies // CORES
    half = zs // 2
    share = rows // xs
    chunks = columns // LANES
    patches = PATCH_DEV * skies

    targets = patch_lists.reshape(entries, 1)
    named = targets == jnp.arange(patches, dtype=jnp.int32)[None, :]
    number = jnp.arange(entries, dtype=jnp.int32)[:, None]
    lowest = jnp.min(jnp.where(named, number, entries), axis=0)
    highest = jnp.max(jnp.where(named, number, -1), axis=0)
    table = jnp.stack([lowest, jnp.where(highest > lowest, highest, entries)])

    bits = clip_bits.reshape(entries, xs, chunks, LANES).transpose(1, 2, 0, 3)
    tiles = visit_tiles.reshape(visits, blocks * rows, columns)

    dims = (visits, blocks, rows, columns, xs, zs)
    out = jax.ShapeDtypeStruct((2, PATCH_DEV, share, columns), jnp.float32)
    any_spec = pl.BlockSpec(memory_space=pl.ANY)
    vmem_spec = pl.BlockSpec(memory_space=pltpu.VMEM)
    dma = pltpu.SemaphoreType.DMA
    message = (FIELDS, 2, share, LANES)
    return pl.pallas_call(
        functools.partial(kernel_body, dims),
        out_shape=(out, out),
        in_specs=[
            any_spec,
            any_spec,
            pl.BlockSpec(memory_space=pltpu.SMEM),
            any_spec,
            any_spec,
        ],
        out_specs=(vmem_spec, vmem_spec),
        scratch_shapes=[
            pltpu.VMEM((visits, blocks * rows, columns), jnp.bfloat16),
            pltpu.VMEM((visits, columns, columns), jnp.bfloat16),
            pltpu.VMEM((xs, CAPACITY, patches), jnp.int32),
            pltpu.SMEM((xs, CAPACITY, patches), jnp.int32),
            *[pltpu.VMEM((xs, entries, share, LANES), jnp.bfloat16)] * chunks,
            *[pltpu.VMEM((xs, entries + 1, share, LANES), jnp.bfloat16)] * chunks,
            *[pltpu.VMEM((xs, entries + 8, LANES), jnp.int32)] * chunks,
            pltpu.VMEM((2, 2, 2) + message, jnp.float32),
            pltpu.VMEM((2, 2) + message, jnp.float32),
            pltpu.VMEM((chunks, half, 2, 2) + message, jnp.float32),
            pltpu.VMEM((chunks, 2) + message, jnp.float32),
            pltpu.VMEM((2, 2, 2) + message, jnp.float32),
            pltpu.VMEM((chunks, half, 2, 2) + message, jnp.float32),
            dma((visits, 2)),
            dma((2, xs)),
            dma((chunks, 2)),
            dma((chunks, visits, xs)),
            dma((chunks, visits, xs)),
            dma((chunks, xs)),
            dma((chunks, xs)),
            dma((2,)),
            dma((chunks, half + 1)),
            dma((2, 2, 2)),
            dma((chunks, half, 2, 2)),
        ],
        compiler_params=pltpu.CompilerParams(
            collective_id=0,
            has_side_effects=True,
            vmem_limit_bytes=66 * 1000 * 1000,
        ),
        name="coadd",
    )(tiles, warp_matrix, flux_scale, bits, table)


def solution(mesh):
    placed = (
        P(("tracts", "sky", "depth"), None, None, None),
        P(("tracts", "sky", "depth"), None, None),
        P(("tracts", "sky", "depth")),
        P(("tracts", "sky", "depth"), None),
        P(("tracts", "sky", "depth"), None, None, None),
    )
    return jax.shard_map(
        per_device,
        mesh=mesh,
        in_specs=placed,
        out_specs=(
            P(None, ("tracts", "sky"), "depth", None),
            P(None, ("tracts", "sky"), "depth", None),
        ),
        check_vma=False,
    )
```

time: 914 us -> 205 us (0.22)
  waiting for transfers between devices: 783 us -> 0 us
  Pallas kernels: 0 us -> 196 us
  other arithmetic: 50.9 us -> 0.68 us
  starting transfers between devices: 40.9 us -> 0 us
  local copies, waits for them, and re-layouts: 28.5 us -> 7.24 us
  matrix products: 10.1 us -> 0 us
    all_to_all x2 -> x0, waiting for transfers between devices: 783 us -> none  [the longest x1 725 us: per_device(): lax.all_to_all(send_tiles, ('sky', 'depth'), split_axis=0, concat_axis=0,...]
    pallas_call x0 -> x1, Pallas kernels: none -> 196 us  [per_device(): pl.pallas_call(functools.partial(kernel_body, dims), out_shape=(out, out)...]
    all_to_all x2 -> x0, starting transfers between devices: 40.9 us -> none  [the longest x1 31.1 us: per_device(): lax.all_to_all(send_bits, ('sky', 'depth'), split_axis=0, concat_axis=0,...]
    reduce_sum x3 -> x0, other arithmetic: 31.4 us -> none  [the longest x1 20.6 us: stack_rows(): shift_square = jnp.sum(keep_both * centred * centred, axis=(0, 2))]
    gather x3 -> x0, local copies, waits for them, and re-layouts: 24.2 us -> none  [the longest x1 15.8 us: per_device(): jnp.take(warped.reshape(entries * depth_size, rows_share, columns), gathe...]
    select_n x4 -> x1, other arithmetic: 17.5 us -> 0.01 us  [per_device(): table = jnp.stack([lowest, jnp.where(highest > lowest, highest, entries)])]
    dot_general x1 -> x0, matrix products: 10.1 us -> none  [per_device(): jnp.einsum('vkrc,vcf->vkrf', visit_tiles, warp_matrix, preferred_element_...]
  transfers between devices with their start and end apart: 2 -> 0, of which waited for: 2 -> 0; matrix products, arithmetic and copies ran while one was open for 4% -> 0% of each run, Pallas kernels for 0% -> 0%
where the time goes in v1:
time: 205 us
  Pallas kernels  196 us (96%)
  local copies, waits for them, and re-layouts  7.24 us (4%)
    pallas_call x1, Pallas kernels, per_device(): pl.pallas_call(functools.partial(kernel_body, dims), out_shape=(out, out)...  196 us

profile of v1, /device:TPU:33, one launch (start us, length us, event | category | flops | bytes accessed | tf_op | source)
XLA Modules:
  0.0 204.9 jit_solution(12502432998360263368)
XLA Ops:
  0.6 1.8 reshape.28
  2.5 1.3 copy.14
  3.8 0.8 eq.15
  4.5 0.1 select_reduce_fusion.1
  4.6 0.6 pad_add_fusion.table_hbm
  5.2 196.3 %coadd.1 = (f32[2,4,16,512]{3,2,1,0:T(8,128)}, f32[2,4,16,512]{3,2,1,0:T(8,128)}) custom-call(bf16[4,2048,512]{2,1,0:T(8,128)(2,1)} %bitcast.8, bf16[4,512,512]{2,1,0:T(8,128)(2,1)} %warp_hbm.1, f32[4]{0:T(128)} %flux.1, s32[4,4,128,128]{3,2,1,0:T(8,128)} %bitcast.9, s32[2,128]{1,0:T(2,128)} %pad_add_fusion.table_hbm), custom_call_target="tpu_custom_call" | custom-call | tf_op jit(solution)/shard_map/coadd/pallas_call | solution.py:377
  201.5 1.7 copy.17
  203.2 1.7 copy.18
  (1 shorter events, 0.0 us)

commit v2 on v1

v2 whole, which is shorter than its diff:
```python
import functools

import jax
import jax.numpy as jnp
from jax import lax
from jax.experimental import pallas as pl
from jax.experimental.pallas import tpu as pltpu
from jax.sharding import PartitionSpec as P

PATCH_DEV = 4
CAPACITY = 2
CORES = 2
LANES = 128
SUBLANES = 8
SUMS = 5
FLOATS = 3
RINGS = 4
COUNT_UNIT = 4096.0
SHIFT_STEPS = 32767.0
RATIO_STEPS = 65535.0
TINY = 1e-37
MESH = pl.DeviceIdType.MESH


def kernel_body(
    dims,
    tiles_hbm,
    warp_hbm,
    flux,
    bits_hbm,
    table_hbm,
    mean_out,
    var_out,
    tiles,
    warp,
    table_v,
    table,
    *refs,
):
    visits, blocks, rows, columns, xs, zs = dims
    entries = visits * blocks
    share = rows // xs
    chunks = columns // LANES
    slabs = share // SUBLANES
    units = chunks * slabs
    half = zs // 2
    rings = min(RINGS, half)
    lead = half // rings
    x_send, x_recv = refs[:units], refs[units : 2 * units]
    bits = refs[2 * units : 2 * units + chunks]
    (
        parts,
        parts_last,
        pair_recv,
        pair_recv_last,
        ring_send,
        ring_recv,
        code_send,
        code_recv,
        load_sem,
        table_sem,
        own_sem,
        x_ssem,
        x_rsem,
        bits_ssem,
        bits_rsem,
        pair_ssem,
        pair_rsem,
        ring_ssem,
        ring_rsem,
    ) = refs[2 * units + chunks :]
    tract = lax.axis_index("tracts")
    sky = lax.axis_index("sky")
    x = lax.axis_index("depth")
    z, core = sky // CORES, lax.rem(sky, CORES)

    def x_peer(dx):
        return lax.rem(x + dx, xs)

    def z_peer(direction):
        step = 1 if direction == 0 else zs - 1
        return (tract, lax.rem(z + step, zs) * CORES + core, x)

    partner = (tract, z * CORES + (1 - core), x)

    barrier = pltpu.get_barrier_semaphore()
    greeted = [(tract, sky, x_peer(dx)) for dx in range(1, xs)]
    greeted += [z_peer(0), z_peer(1), partner]
    for device in greeted:
        pl.semaphore_signal(barrier, inc=1, device_id=device, device_id_type=MESH)

    def load_visit(v):
        return (
            pltpu.make_async_copy(tiles_hbm.at[v], tiles.at[v], load_sem.at[v, 0]),
            pltpu.make_async_copy(warp_hbm.at[v], warp.at[v], load_sem.at[v, 1]),
        )

    for v in range(visits):
        for copy in load_visit(v):
            copy.start()
    for s in range(xs):
        for u in range(units):
            x_recv[u][s, entries] = jnp.zeros((SUBLANES, LANES), jnp.bfloat16)
        for j in range(chunks):
            bits[j][s, pl.ds(entries, 8), :] = jnp.zeros((8, LANES), jnp.int32)
    pl.semaphore_wait(barrier, len(greeted))

    def table_copy(dx):
        return pltpu.make_async_remote_copy(
            src_ref=table_hbm,
            dst_ref=table_v.at[x],
            send_sem=table_sem.at[0, dx],
            recv_sem=table_sem.at[1, dx],
            device_id=(tract, sky, x_peer(dx)),
            device_id_type=MESH,
        )

    def bits_copy(j, dx):
        return pltpu.make_async_remote_copy(
            src_ref=bits_hbm.at[x_peer(dx), j],
            dst_ref=bits[j].at[x, pl.ds(0, entries)],
            send_sem=bits_ssem.at[j, dx],
            recv_sem=bits_rsem.at[j, dx],
            device_id=(tract, sky, x_peer(dx)),
            device_id_type=MESH,
        )

    def x_copies(u, dx):
        pieces = visits if u == 0 else 1
        size = entries // pieces
        return [
            pltpu.make_async_remote_copy(
                src_ref=x_send[u].at[x_peer(dx), pl.ds(n * size, size)],
                dst_ref=x_recv[u].at[x, pl.ds(n * size, size)],
                send_sem=x_ssem.at[u, n, dx],
                recv_sem=x_rsem.at[u, n, dx],
                device_id=(tract, sky, x_peer(dx)),
                device_id_type=MESH,
            )
            for n in range(pieces)
        ]

    def own_bits(j):
        return pltpu.make_async_copy(
            bits_hbm.at[x, j], bits[j].at[x, pl.ds(0, entries)], own_sem.at[units + j]
        )

    def own_rows(u):
        return pltpu.make_async_copy(
            x_send[u].at[x], x_recv[u].at[x, pl.ds(0, entries)], own_sem.at[u]
        )

    own_table = pltpu.make_async_copy(table_hbm, table_v.at[x], table_sem.at[0, 0])
    own_table.start()
    for dx in range(1, xs):
        table_copy(dx).start()

    group = 8
    for j in range(chunks):
        own_bits(j).start()
        for dx in range(1, xs):
            bits_copy(j, dx).start()
        for v in range(visits):
            if j == 0:
                for copy in load_visit(v):
                    copy.wait()
            weights = warp[v, :, pl.ds(j * LANES, LANES)]
            scale = flux[v]

            def multiply(n, carry):
                first = pl.multiple_of(n * (group * rows), group * rows)
                product = jnp.dot(
                    tiles[v, pl.ds(first, group * rows), :],
                    weights,
                    preferred_element_type=jnp.float32,
                )
                scaled = (product * scale).reshape(group, xs, slabs, SUBLANES, LANES)
                at = pl.ds(v * blocks + n * group, group)
                for d in range(xs):
                    for slab in range(slabs):
                        x_send[j * slabs + slab][d, at] = scaled[:, d, slab].astype(
                            jnp.bfloat16
                        )
                return carry

            lax.fori_loop(0, blocks // group, multiply, 0)
            if j == 0:
                for dx in range(1, xs):
                    x_copies(0, dx)[v].start()
        for u in range(j * slabs, (j + 1) * slabs):
            if u > 0:
                for dx in range(1, xs):
                    x_copies(u, dx)[0].start()
            own_rows(u).start()

    own_table.wait()
    for dx in range(1, xs):
        table_copy(dx).wait()
    to_scalar = pltpu.make_async_copy(table_v, table, table_sem.at[1, 0])
    to_scalar.start()
    to_scalar.wait()

    def wait_unit(u):
        if u % slabs == 0:
            own_bits(u // slabs).wait()
            for dx in range(1, xs):
                bits_copy(u // slabs, dx).wait_recv()
        own_rows(u).wait()
        for dx in range(1, xs):
            for copy in x_copies(u, dx):
                copy.wait_recv()

    def wait_unit_sent(u):
        for dx in range(1, xs):
            if u % slabs == 0:
                bits_copy(u // slabs, dx).wait_send()
            for copy in x_copies(u, dx):
                copy.wait_send()

    row = lax.broadcasted_iota(jnp.int32, (SUBLANES, LANES), 0)
    zero = jnp.zeros((SUBLANES, LANES), jnp.float32)

    def patch_sums(u, patch):
        j, slab = u // slabs, u % slabs
        mask_first = jnp.left_shift(jnp.int32(1), row + slab * SUBLANES)
        mask_both = jnp.bitwise_or(
            mask_first, jnp.left_shift(jnp.int32(1), row + (16 + slab * SUBLANES))
        )

        def source(s, sums):
            count, s1, q1, sb, qb = sums
            for r in range(CAPACITY):
                e = table[s, r, patch]
                sample = x_recv[u][s, e].astype(jnp.float32)
                word = bits[j][s, pl.ds(e, 1), :]
                first = jnp.bitwise_and(word, mask_first) != 0
                both = jnp.bitwise_and(word, mask_both) == mask_both
                kept = jnp.where(first, sample, 0.0)
                s1 = s1 + kept
                q1 = q1 + kept * kept
                kept = jnp.where(both, sample, 0.0)
                sb = sb + kept
                qb = qb + kept * kept
                count = count + jnp.where(
                    both, 1.0 + COUNT_UNIT, jnp.where(first, 1.0, 0.0)
                )
            return count, s1, q1, sb, qb

        return lax.fori_loop(0, xs, source, (zero,) * SUMS, unroll=True)

    def ring_slot(u):
        return lax.rem(u, rings)

    def pair_copy(u, k):
        return pltpu.make_async_remote_copy(
            src_ref=parts.at[ring_slot(u), 0],
            dst_ref=pair_recv.at[ring_slot(u), k],
            send_sem=pair_ssem.at[ring_slot(u)],
            recv_sem=pair_rsem.at[ring_slot(u), k],
            device_id=partner,
            device_id_type=MESH,
        )

    def pair_copy_last(u):
        return pltpu.make_async_remote_copy(
            src_ref=parts_last.at[0],
            dst_ref=pair_recv_last.at[ring_slot(u)],
            send_sem=pair_ssem.at[rings],
            recv_sem=pair_rsem.at[ring_slot(u), half],
            device_id=partner,
            device_id_type=MESH,
        )

    def store_group(dst, at, u, group):
        def two(h, carry):
            for q in range(2):
                sums = patch_sums(u, group * PATCH_DEV + 2 * h + q)
                for f, value in enumerate(sums):
                    dst[at + (h, f, q)] = value
            return carry

        lax.fori_loop(0, PATCH_DEV // 2, two, 0, unroll=True)

    def partials(u, k):
        if not (isinstance(k, int) and k == 0):
            pair_copy(u, k - 1).wait_send()
        forth = lax.rem(z + (half - k), zs) * CORES
        back = lax.rem(z + (half + k), zs) * CORES

        def one(n, carry):
            w, direction = jnp.right_shift(n, 1), jnp.bitwise_and(n, 1)
            which = jnp.where(w == 0, 1 - core, core)
            group = jnp.where(direction == 0, forth, back) + which
            store_group(parts, (ring_slot(u), w, direction), u, group)

            @pl.when(n == 1)
            def _():
                pair_copy(u, k).start()

            return carry

        lax.fori_loop(0, 2 * CORES, one, 0)

    def partials_last(u):
        pair_copy(u, half - 1).wait_send()
        if half > 1:
            wait_ring_sent(u, half - 2, half == 2)

        def one(w, carry):
            which = jnp.where(w == 0, 1 - core, core)
            store_group(parts_last, (w,), u, z * CORES + which)

            @pl.when(w == 0)
            def _():
                pair_copy_last(u).start()

            return carry

        lax.fori_loop(0, CORES, one, 0)

    def counts(packed):
        both = jnp.floor(packed * (1.0 / COUNT_UNIT))
        return packed - both * COUNT_UNIT, both

    def encode(packed, s1, q1, sb, qb):
        c1, cb = counts(packed)
        mean = s1 / jnp.maximum(c1, 1.0)
        mean_both = sb / jnp.maximum(cb, 1.0)
        m1 = jnp.maximum(q1 - s1 * mean, 0.0)
        mb = jnp.maximum(qb - sb * mean_both, 0.0)
        unit = lax.rsqrt(jnp.maximum(m1, TINY))
        shift = (mean_both - mean) * jnp.sqrt(cb) * unit
        shift = jnp.clip(shift, -1.0, 1.0) * SHIFT_STEPS
        ratio = jnp.minimum(mb * unit * unit, 1.0) * RATIO_STEPS
        code = jnp.bitwise_or(
            jnp.left_shift(jnp.floor(shift + 0.5).astype(jnp.int32), 16),
            jnp.floor(ratio + 0.5).astype(jnp.int32),
        )
        return (packed, s1, m1), code

    def decode(packed, s1, m1, code):
        c1, cb = counts(packed)
        mean = s1 / jnp.maximum(c1, 1.0)
        shift = jnp.right_shift(code, 16).astype(jnp.float32) * (1.0 / SHIFT_STEPS)
        ratio = jnp.bitwise_and(code, 65535).astype(jnp.float32) * (1.0 / RATIO_STEPS)
        spread = jnp.sqrt(m1) * lax.rsqrt(jnp.maximum(cb, 1.0))
        mean_both = mean + shift * spread
        sb = cb * mean_both
        return packed, s1, m1 + s1 * mean, sb, ratio * m1 + sb * mean_both

    def ring_copies(u, k, direction, h):
        par = ring_slot(u)
        return [
            pltpu.make_async_remote_copy(
                src_ref=send.at[par, lax.rem(k, 2), direction, h],
                dst_ref=recv.at[par, k, direction, h],
                send_sem=ring_ssem.at[par, lax.rem(k, 2), direction, h, kind],
                recv_sem=ring_rsem.at[par, k, direction, h, kind],
                device_id=z_peer(direction),
                device_id_type=MESH,
            )
            for kind, (send, recv) in enumerate(
                ((ring_send, ring_recv), (code_send, code_recv))
            )
        ]

    def wait_ring(u, k, direction, h):
        for copy in ring_copies(u, k, direction, h):
            copy.wait_recv()

    def wait_ring_sent(u, k, outset=False):
        for h in range(2):
            for direction in range(2):
                if not outset or direction == h:
                    for copy in ring_copies(u, k, direction, h):
                        copy.wait_send()

    def received(u, k, direction, h):
        at = (ring_slot(u), k, direction, h)
        return decode(*(ring_recv[at + (f,)] for f in range(FLOATS)), code_recv[at])

    def tick(u, k, stage):
        par = ring_slot(u)
        pair_copy(u, k).wait_recv()
        if stage > 1:

            @pl.when(k > 2)
            def _():
                wait_ring_sent(u, k - 2)

            @pl.when(k == 2)
            def _():
                wait_ring_sent(u, 0, True)

        for h in range(2):
            going = [d for d in range(2) if stage > 0 or d == h]
            coming = [d for d in range(2) if stage > 1 or (stage == 1 and d == h)]
            for direction in coming:
                wait_ring(u, k - 1, direction, h)
            ready = []
            for direction in going:
                sums = [
                    parts[par, 1, direction, h, f] + pair_recv[par, k, direction, h, f]
                    for f in range(SUMS)
                ]
                if direction in coming:
                    earlier = received(u, k - 1, direction, h)
                    sums = [a + b for a, b in zip(sums, earlier)]
                ready.append(encode(*sums))
            for direction, (floats, code) in zip(going, ready):
                for f in range(FLOATS):
                    ring_send[par, lax.rem(k, 2), direction, h, f] = floats[f]
                code_send[par, lax.rem(k, 2), direction, h] = code
            for direction in going:
                for copy in ring_copies(u, k, direction, h):
                    copy.start()

    def finish(u):
        pair_copy_last(u).wait()
        wait_ring_sent(u, half - 1, half == 1)
        row_at = pl.multiple_of(lax.rem(u, slabs) * SUBLANES, SUBLANES)
        rows_at = pl.ds(row_at, SUBLANES)
        lanes = pl.ds(pl.multiple_of(lax.div(u, slabs) * LANES, LANES), LANES)
        for h in range(2):
            total = [
                parts_last[1, h, f] + pair_recv_last[ring_slot(u), h, f] for f in range(SUMS)
            ]
            for direction in range(2):
                if half > 1 or direction == h:
                    wait_ring(u, half - 1, direction, h)
                    earlier = received(u, half - 1, direction, h)
                    total = [a + b for a, b in zip(total, earlier)]
            packed, s1, q1, sb, qb = total
            count_first, count_both = counts(packed)
            first_mean = s1 / jnp.maximum(count_first, 1.0)
            first_var = (q1 - s1 * first_mean) / jnp.maximum(count_first - 1.0, 1.0)
            shift_sum = sb - first_mean * count_both
            shift_square = qb - first_mean * (sb + shift_sum)
            move = shift_sum / jnp.maximum(count_both, 1.0)
            final_var = (shift_square - shift_sum * move) / jnp.maximum(
                count_both - 1.0, 1.0
            )
            at = pl.ds(2 * h, 2)
            mean_out[0, at, rows_at, lanes] = first_mean
            mean_out[1, at, rows_at, lanes] = first_mean + move
            var_out[0, at, rows_at, lanes] = first_var
            var_out[1, at, rows_at, lanes] = final_var

    def advance(u, k):
        @pl.when(k == 0)
        def _():
            tick(u, 0, 0)

        if half > 1:

            @pl.when(k == 1)
            def _():
                tick(u, 1, 1)

        if half > 2:

            @pl.when(k > 1)
            def _():
                tick(u, k, 2)

        for i in range(units):

            @pl.when(jnp.logical_and(u == i, k + 1 < half))
            def _():
                partials(i, k + 1)

            @pl.when(jnp.logical_and(u == i, k + 1 == half))
            def _():
                partials_last(i)

    def arrive(a):
        for i in range(units):

            @pl.when(a == i)
            def _():
                wait_unit(i)
                partials(i, 0)

    def segment(a, outer):
        def step(k, middle):
            @pl.when(jnp.logical_and(k == lead - 1, a >= rings))
            def _():
                finish(a - rings)

            def ring(m, inner):
                r = rings - 1 - m
                u = a - r

                @pl.when(jnp.logical_and(k == 0, r == min(1, rings - 1)))
                def _():
                    arrive(a)

                @pl.when(jnp.logical_and(u >= 0, u < units))
                def _():
                    advance(u, r * lead + k)

                return inner

            return lax.fori_loop(0, rings, ring, middle)

        return lax.fori_loop(0, lead, step, outer)

    lax.fori_loop(0, units + rings, segment, 0)
    for u in range(units):
        wait_unit_sent(u)


def per_device(visit_tiles, warp_matrix, flux_scale, patch_lists, clip_bits):
    visits, blocks, rows, columns = visit_tiles.shape
    entries = visits * blocks
    xs = lax.axis_size("depth")
    skies = lax.axis_size("sky")
    zs = skies // CORES
    half = zs // 2
    share = rows // xs
    chunks = columns // LANES
    patches = PATCH_DEV * skies

    targets = patch_lists.reshape(entries, 1)
    named = targets == jnp.arange(patches, dtype=jnp.int32)[None, :]
    number = jnp.arange(entries, dtype=jnp.int32)[:, None]
    lowest = jnp.min(jnp.where(named, number, entries), axis=0)
    highest = jnp.max(jnp.where(named, number, -1), axis=0)
    table = jnp.stack([lowest, jnp.where(highest > lowest, highest, entries)])

    bits = clip_bits.reshape(entries, xs, chunks, LANES).transpose(1, 2, 0, 3)
    tiles = visit_tiles.reshape(visits, blocks * rows, columns)

    dims = (visits, blocks, rows, columns, xs, zs)
    out = jax.ShapeDtypeStruct((2, PATCH_DEV, share, columns), jnp.float32)
    any_spec = pl.BlockSpec(memory_space=pl.ANY)
    vmem_spec = pl.BlockSpec(memory_space=pltpu.VMEM)
    dma = pltpu.SemaphoreType.DMA
    slabs = share // SUBLANES
    units = chunks * slabs
    unit = (SUBLANES, LANES)
    sums = (SUMS, 2) + unit
    floats = (FLOATS, 2) + unit
    rings = min(RINGS, half)
    return pl.pallas_call(
        functools.partial(kernel_body, dims),
        out_shape=(out, out),
        in_specs=[
            any_spec,
            any_spec,
            pl.BlockSpec(memory_space=pltpu.SMEM),
            any_spec,
            any_spec,
        ],
        out_specs=(vmem_spec, vmem_spec),
        scratch_shapes=[
            pltpu.VMEM((visits, blocks * rows, columns), jnp.bfloat16),
            pltpu.VMEM((visits, columns, columns), jnp.bfloat16),
            pltpu.VMEM((xs, CAPACITY, patches), jnp.int32),
            pltpu.SMEM((xs, CAPACITY, patches), jnp.int32),
            *[pltpu.VMEM((xs, entries) + unit, jnp.bfloat16)] * units,
            *[pltpu.VMEM((xs, entries + 1) + unit, jnp.bfloat16)] * units,
            *[pltpu.VMEM((xs, entries + 8, LANES), jnp.int32)] * chunks,
            pltpu.VMEM((rings, 2, 2, 2) + sums, jnp.float32),
            pltpu.VMEM((2, 2) + sums, jnp.float32),
            pltpu.VMEM((rings, half, 2, 2) + sums, jnp.float32),
            pltpu.VMEM((rings, 2) + sums, jnp.float32),
            pltpu.VMEM((rings, 2, 2, 2) + floats, jnp.float32),
            pltpu.VMEM((rings, half, 2, 2) + floats, jnp.float32),
            pltpu.VMEM((rings, 2, 2, 2, 2) + unit, jnp.int32),
            pltpu.VMEM((rings, half, 2, 2, 2) + unit, jnp.int32),
            dma((visits, 2)),
            dma((2, xs)),
            dma((units + chunks,)),
            dma((units, visits, xs)),
            dma((units, visits, xs)),
            dma((chunks, xs)),
            dma((chunks, xs)),
            dma((rings + 1,)),
            dma((rings, half + 1)),
            dma((rings, 2, 2, 2, 2)),
            dma((rings, half, 2, 2, 2)),
        ],
        compiler_params=pltpu.CompilerParams(
            collective_id=0,
            has_side_effects=True,
            vmem_limit_bytes=66 * 1000 * 1000,
        ),
        name="coadd",
    )(tiles, warp_matrix, flux_scale, bits, table)


def solution(mesh):
    placed = (
        P(("tracts", "sky", "depth"), None, None, None),
        P(("tracts", "sky", "depth"), None, None),
        P(("tracts", "sky", "depth")),
        P(("tracts", "sky", "depth"), None),
        P(("tracts", "sky", "depth"), None, None, None),
    )
    return jax.shard_map(
        per_device,
        mesh=mesh,
        in_specs=placed,
        out_specs=(
            P(None, ("tracts", "sky"), "depth", None),
            P(None, ("tracts", "sky"), "depth", None),
        ),
        check_vma=False,
    )
```

time: 205 us -> 181 us (0.88); the launches traced: 205 us -> 178 us
  Pallas kernels: 196 us -> 169 us
    pallas_call x1, Pallas kernels: 196 us -> 169 us  [per_device(): pl.pallas_call(functools.partial(kernel_body, dims), out_shape=(out, out)...]
where the time goes in v2:
time: 181 us; the launch traced here: 178 us
  Pallas kernels  169 us (93%)
  local copies, waits for them, and re-layouts  7.24 us (4%)
    pallas_call x1, Pallas kernels, per_device(): pl.pallas_call(functools.partial(kernel_body, dims), out_shape=(out, out)...  169 us

profile of v2, /device:TPU:33, one launch (start us, length us, event | category | flops | bytes accessed | tf_op | source)
XLA Modules:
  0.0 177.7 jit_solution(994178014787226997)
XLA Ops:
  0.6 1.8 %reshape.28 = s32[128,4,4,128]{3,2,1,0:T(4,128)S(1)} reshape(s32[4,32,4,512]{3,2,1,0:T(4,128)} %param.9) | data formatting | bytes 2097152 | tf_op jit(solution)/shard_map/reshape | solution.py:531
  2.5 1.3 copy.14
  3.8 0.8 eq.15
  4.5 0.1 select_reduce_fusion.1
  4.6 0.6 pad_add_fusion.table_hbm
  5.2 169.1 %coadd.1 = (f32[2,4,16,512]{3,2,1,0:T(8,128)}, f32[2,4,16,512]{3,2,1,0:T(8,128)}) custom-call(bf16[4,2048,512]{2,1,0:T(8,128)(2,1)} %bitcast.8, bf16[4,512,512]{2,1,0:T(8,128)(2,1)} %warp_hbm.1, f32[4]{0:T(128)} %flux.1, s32[4,4,128,128]{3,2,1,0:T(8,128)} %bitcast.9, s32[2,128]{1,0:T(2,128)} %pad_add_fusion.table_hbm), custom_call_target="tpu_custom_call" | custom-call | tf_op jit(solution)/shard_map/coadd/pallas_call | solution.py:545
  174.4 1.7 copy.17
  176.0 1.7 copy.18
  (1 shorter events, 0.0 us)

commit v3 on v2

--- a/solution.py
+++ b/solution.py
@@ -45,7 +45,7 @@
     units = chunks * slabs
     half = zs // 2
     rings = min(RINGS, half)
-    lead = half // rings
+    lead = -(-half // rings)
     x_send, x_recv = refs[:units], refs[units : 2 * units]
     bits = refs[2 * units : 2 * units + chunks]
     (
@@ -117,7 +117,7 @@
 
     def bits_copy(j, dx):
         return pltpu.make_async_remote_copy(
-            src_ref=bits_hbm.at[x_peer(dx), j],
+            src_ref=bits_hbm.at[:, x_peer(dx), pl.ds(j * LANES, LANES)],
             dst_ref=bits[j].at[x, pl.ds(0, entries)],
             send_sem=bits_ssem.at[j, dx],
             recv_sem=bits_rsem.at[j, dx],
@@ -142,7 +142,7 @@
 
     def own_bits(j):
         return pltpu.make_async_copy(
-            bits_hbm.at[x, j], bits[j].at[x, pl.ds(0, entries)], own_sem.at[units + j]
+            bits_hbm.at[:, x, pl.ds(j * LANES, LANES)], bits[j].at[x, pl.ds(0, entries)], own_sem.at[units + j]
         )
 
     def own_rows(u):
@@ -483,7 +483,7 @@
 
     def segment(a, outer):
         def step(k, middle):
-            @pl.when(jnp.logical_and(k == lead - 1, a >= rings))
+            @pl.when(jnp.logical_and(k == min(1, lead - 1), a >= rings))
             def _():
                 finish(a - rings)
 
@@ -495,7 +495,9 @@
                 def _():
                     arrive(a)
 
-                @pl.when(jnp.logical_and(u >= 0, u < units))
+                going = jnp.logical_and(u >= 0, u < units)
+
+                @pl.when(jnp.logical_and(going, r * lead + k < half))
                 def _():
                     advance(u, r * lead + k)
 
@@ -528,7 +530,7 @@
     highest = jnp.max(jnp.where(named, number, -1), axis=0)
     table = jnp.stack([lowest, jnp.where(highest > lowest, highest, entries)])
 
-    bits = clip_bits.reshape(entries, xs, chunks, LANES).transpose(1, 2, 0, 3)
+    bits = clip_bits.reshape(entries, xs, columns)
     tiles = visit_tiles.reshape(visits, blocks * rows, columns)
 
     dims = (visits, blocks, rows, columns, xs, zs)

time: 181 us -> 178 us (0.983)
  local copies, waits for them, and re-layouts: 7.24 us -> 4.11 us
    reshape x2 -> x0, local copies, waits for them, and re-layouts: 3.14 us -> none  [per_device(): bits = clip_bits.reshape(entries, xs, chunks, LANES).transpose(1, 2, 0, 3)]
where the time goes in v3:
time: 178 us; the launch traced here: 175 us
  Pallas kernels  169 us (95%)
  local copies, waits for them, and re-layouts  4.11 us (2%)
    pallas_call x1, Pallas kernels, per_device(): pl.pallas_call(functools.partial(kernel_body, dims), out_shape=(out, out)...  169 us

profile of v3, /device:TPU:33, one launch (start us, length us, event | category | flops | bytes accessed | tf_op | source)
XLA Modules:
  0.0 174.6 jit_solution(13735602644833158967)
XLA Ops:
  0.6 0.8 eq.15
  1.4 0.1 select_reduce_fusion.1
  1.5 0.6 pad_add_fusion.table_hbm
  2.1 169.1 %coadd.1 = (f32[2,4,16,512]{3,2,1,0:T(8,128)}, f32[2,4,16,512]{3,2,1,0:T(8,128)}) custom-call(bf16[4,2048,512]{2,1,0:T(8,128)(2,1)} %bitcast.6, bf16[4,512,512]{2,1,0:T(8,128)(2,1)} %warp_hbm.1, f32[4]{0:T(128)} %flux.1, s32[128,4,512]{2,1,0:T(4,128)} %bitcast.7, s32[2,128]{1,0:T(2,128)} %pad_add_fusion.table_hbm), custom_call_target="tpu_custom_call" | custom-call | tf_op jit(solution)/shard_map/coadd/pallas_call | solution.py:547
  171.2 1.7 copy.9
  172.9 1.7 copy.10
  (1 shorter events, 0.0 us)
